TPU v7x, 32 devices: a whole 2x2x4 slice. The times are simulated.
32 devices in a mesh: rep: 2 (over x), px: 4 (over y, core), py: 4 (over z).
Axes of the slice: x: 2, y: 2, z: 4, core: 2. Of those that a mesh axis runs over, the one named last changes fastest.
Arguments:
- density: float32 [4, 128, 128, 128], P('rep', 'px', 'py'), parts along dimension 0, may hold values from -6 to 6
- kernel_factors: float32 [3, 89, 256], replicated, as said below
Outputs:
- potential: float32 [4, 128, 128, 128], P('rep', 'px', 'py'), parts along dimension 0
There are 2 independent parts, one for each index of `rep`. A program takes and returns all parts, laid end to end along the dimension named above; an argument that names none is the same for every part. Nothing has to cross between parts.
Inputs may be any that keep to these rules, and one draw needn't show every extreme that they name: Each factor is even in its frequency, kernel_factors[d, g, k] = kernel_factors[d, g, 256 - k], and is zero at k = 128.
All inputs are finite; a program needn't handle non-finite values.
Results may differ from a plain program's by a relative error of at most 0.00005.
Values sent between devices are 32-bit elements; how exact they have to be, the bound alone decides.
A program may use at most 128 MiB of HBM per device.

v0:
```python
import math
import jax
import jax.numpy as jnp
import numpy as np
from jax import lax
from jax.sharding import PartitionSpec as P

HIGH = lax.Precision.HIGH


def spectral_table(length, chunks):
    freq = np.arange(length).reshape(chunks, 1, length // chunks, 1)
    angle = freq * np.arange(length) % (2 * length) * (math.pi / length)
    both = np.concatenate([np.cos(angle), np.sin(angle)], 1)
    return both.reshape(2 * length, length).astype(np.float32)


def dot(spec, left, right):
    return jnp.einsum(spec, left, right, precision=HIGH, preferred_element_type=jnp.float32)


def kernel_block(factors, y_start, y_count, z_start, z_count):
    length = factors.shape[2] // 2
    weights = np.full((length,), 1.0 / length, np.float32)
    weights[0] = 0.5 / length
    factors = factors[:, :, :length] * weights
    factor_y = lax.dynamic_slice_in_dim(factors[1], y_start, y_count, 1)
    factor_z = lax.dynamic_slice_in_dim(factors[2], z_start, z_count, 1)
    pair = factor_z[:, :, None] * factor_y[:, None, :]
    return jnp.einsum("gzy,gx->zyx", pair, factors[0], precision=lax.Precision.HIGHEST)


def body(density, kernel_factors):
    replicas, rows_x, rows_y, length = density.shape
    count_px = lax.axis_size("px")
    count_py = lax.axis_size("py")
    half = count_px // replicas
    trade = [[i + half * r for r in range(replicas)] for i in range(half)]
    lines = [[r * half + i for i in range(half)] for r in range(replicas)]
    index_x = lax.axis_index("px") % half
    index_y = lax.axis_index("py")
    table_z = spectral_table(length, count_py)
    table_y = spectral_table(length, half)
    order = np.arange(length).reshape(replicas, half, rows_x).transpose(1, 0, 2).reshape(-1)
    table_x = spectral_table(length, 1)[:, order]
    held = lax.all_to_all(density, "px", 0, 0, axis_index_groups=trade, tiled=True)
    held = held.reshape(replicas * rows_x, rows_y, length)
    held = dot("kz,xyz->kyx", table_z, held)
    held = lax.all_to_all(held, "py", 0, 1, tiled=True)
    held = dot("qy,kyx->kqx", table_y, held)
    held = lax.all_to_all(held, "px", 1, 2, axis_index_groups=lines, tiled=True)
    z_freq, y_freq = (length // count_py, length // half)
    kernel = kernel_block(kernel_factors, index_x * y_freq, y_freq, index_y * z_freq, z_freq)
    held = dot("kqx,px->kqp", held, table_x)
    held = held.reshape(2, z_freq, 2, y_freq, 2, length) * kernel[None, :, None, :, None, :]
    held = held.reshape(2 * z_freq, 2 * y_freq, 2 * length)
    held = dot("kqp,px->kqx", held, table_x)
    held = lax.all_to_all(held, "px", 2, 1, axis_index_groups=lines, tiled=True)
    held = dot("kqx,qy->kyx", held, table_y)
    held = lax.all_to_all(held, "py", 1, 0, tiled=True)
    held = dot("kyx,kz->xyz", held, table_z)
    held = held.reshape(replicas, rows_x, rows_y, length)
    return lax.all_to_all(held, "px", 0, 0, axis_index_groups=trade, tiled=True)


def solution(mesh):
    placed = (P("rep", "px", "py", None), P())
    return jax.shard_map(
        body, mesh=mesh, in_specs=placed, out_specs=P("rep", "px", "py", None), check_vma=False
    )
```

profile of v0, /device:TPU:0, one launch (start us, length us, event | category | flops | bytes accessed | tf_op | source)
XLA Modules:
  0.0 359.6 jit_solution(2208279922184418932)
XLA Ops:
  0.0 18.8 %all_to_all.79 = f32[2,32,32,128]{3,2,1,0:T(8,128)S(1)} all-to-all(f32[2,32,32,128]{3,2,1,0:T(8,128)} %param.9), channel_id=1, replica_groups={{0,8},{4,12},{1,9},{5,13},{2,10},{6,14},{3,11},{7,15},{16,24},{20,28},{..., dimensions={0} | all-to-all | bytes 2097152 | tf_op jit(solution)/shard_map/all_to_all | solution.py:46
  18.8 0.6 copy.26
  19.4 0.0 copy-done.4
  19.4 1.0 convolution_bitcast_fusion.2
  20.4 4.5 %copy.27 = f32[256,32,64]{2,1,0:T(8,128)} copy(f32[256,32,64]{0,2,1:T(8,128)S(1)} %convolution_bitcast_fusion.2) | data formatting | bytes 4194304 | tf_op jit(solution)/shard_map/kz,xyz->kyx/transpose | solution.py:19
  24.9 5.5 %reshape.41 = f32[4,1,131072]{2,1,0:T(1,128)} reshape(f32[256,32,64]{2,1,0:T(8,128)} %copy.27) | data formatting | bytes 4194304
  30.4 5.3 %all-to-all-start.1 = ((f32[4,1,131072]{2,1,0:T(1,128)}), f32[4,1,131072]{2,1,0:T(1,128)S(1)}, u32[]{:S(2)}, u32[]{:S(2)}) async-start(f32[4,1,131072]{2,1,0:T(1,128)} %reshape.41), calls=%async_computation.1 | async-start | bytes 4194304 | tf_op jit(solution)/shard_map/all_to_all | solution.py:49
  35.7 0.0 copy-done.7
  35.8 0.0 copy-done.8
  35.8 0.1 constant_dynamic-slice_fusion.1
  35.9 0.1 copy.32
  36.0 0.1 constant_dynamic-slice_fusion
  36.0 0.1 copy.33
  36.1 1.0 fusion.6
  37.1 45.8 %all-to-all-done.1 = f32[4,1,131072]{2,1,0:T(1,128)S(1)} async-done(((f32[4,1,131072]{2,1,0:T(1,128)}), f32[4,1,131072]{2,1,0:T(1,128)S(1)}, u32[]{:S(2)}, u32[]{:S(2)}) %all-to-all-start.1) | async-done | bytes 2097184 | tf_op jit(solution)/shard_map/all_to_all | solution.py:49
  82.9 1.3 copy-done
  84.2 0.5 broadcast.3
  84.7 7.7 %reduce = f32[4,131072]{1,0:T(4,128)S(1)} reduce(f32[4,1,131072]{2,1,0:T(1,128)} %copy-done, f32[]{:T(128)} %broadcast.3), dimensions={1}, to_apply=%all_to_all.57.reduce_sub_computation | reduce | bytes 4194308 | tf_op jit(solution)/shard_map/all_to_all | solution.py:49
  92.4 3.9 %reshape.42 = f32[256,32,64]{2,1,0:T(8,128)} reshape(f32[4,131072]{1,0:T(4,128)S(1)} %reduce) | data formatting | bytes 4194304
  96.4 2.9 copy.28
  99.2 5.9 %convolution_bitcast_fusion = f32[64,256,64]{1,2,0:T(8,128)} fusion(f32[64,128,64]{2,1,0:T(8,128)S(1)} %bitcast.56, f32[256,128,1]{1,0,2:T(8,128)S(1)} %copy-done.3), kind=kOutput, calls=%fused_computation.6 | convolution fusion | flops 805306368 | bytes 6422528 | tf_op jit(solution)/shard_map/qy,kyx->kqx/dot_general | solution.py:19
  105.1 9.2 %copy.30 = f32[64,256,64]{2,0,1:T(8,128)} copy(f32[64,256,64]{1,2,0:T(8,128)} %convolution_bitcast_fusion) | data formatting | bytes 8388608 | tf_op jit(solution)/shard_map/qy,kyx->kqx/transpose | solution.py:19
  114.3 8.7 %reshape.43 = f32[2,1,524288]{2,1,0:T(1,128)} reshape(f32[256,64,64]{2,1,0:T(8,128)} %bitcast.52) | data formatting | bytes 8388608
  123.0 11.9 %all_to_all.80 = f32[2,1,524288]{2,1,0:T(1,128)} all-to-all(f32[2,1,524288]{2,1,0:T(1,128)} %reshape.43), channel_id=1, replica_groups={{0,4},{8,12},{1,5},{9,13},{2,6},{10,14},{3,7},{11,15},{16,20},{24,28},{..., dimensions={0} | all-to-all | bytes 8388608 | tf_op jit(solution)/shard_map/all_to_all | solution.py:51
  134.8 16.5 %reduce.1 = f32[2,524288]{1,0:T(2,128)} reduce(f32[2,1,524288]{2,1,0:T(1,128)} %all_to_all.80, f32[]{:T(128)} %broadcast.3), dimensions={1}, to_apply=%all_to_all.61.reduce_sub_computation | reduce | bytes 8388612 | tf_op jit(solution)/shard_map/all_to_all | solution.py:51
  151.3 9.9 %reshape.44 = f32[256,64,64]{2,1,0:T(8,128)} reshape(f32[2,524288]{1,0:T(2,128)} %reduce.1) | data formatting | bytes 8388608
  161.3 15.3 %copy.49 = f32[64,2,128,64]{3,1,2,0:T(2,128)} copy(f32[64,2,128,64]{3,0,2,1:T(8,128)} %bitcast.53) | data formatting | bytes 8388608 | tf_op jit(solution)/shard_map/all_to_all | solution.py:51
  176.6 9.0 %reshape.34 = f32[2,32,2,64,128,1]{4,3,2,1,0,5:T(8,128)} reshape(f32[64,128,2,64]{3,2,1,0:T(2,128)} %bitcast.54) | data formatting | bytes 8388608 | tf_op jit(solution)/shard_map/kqx,px->kqp/dot_general | solution.py:19
  185.6 5.6 %broadcast_multiply_fusion = f32[2,32,2,64,2,128]{5,3,4,2,1,0:T(8,128)S(1)} fusion(f32[32,64,128]{2,1,0:T(8,128)S(1)} %fusion.6, f32[2,128,128,1,1,1]{2,1,0,5,4,3:T(8,128)S(1)} %copy-done.2, f32[2,32,2,64,128,1]{4,3,2,1,0,5:T(8,128)} %reshape.34), kind=kOutput, calls=%fused_computation.5 | convolution fusion | flops 1612709888 | bytes 13762560 | tf_op jit(solution)/shard_map/kqx,px->kqp/dot_general | solution.py:19
  191.1 7.7 %copy.34 = f32[2,32,2,64,2,128]{5,4,3,2,1,0:T(2,128)} copy(f32[2,32,2,64,2,128]{5,3,4,2,1,0:T(8,128)S(1)} %broadcast_multiply_fusion) | data formatting | bytes 16777216 | tf_op jit(solution)/shard_map/mul | solution.py:55
  198.9 11.5 %reshape.22 = f32[64,128,256]{2,1,0:T(8,128)} reshape(f32[2,32,2,64,2,128]{5,4,3,2,1,0:T(2,128)} %copy.34) | data formatting | bytes 16777216 | tf_op jit(solution)/shard_map/reshape | solution.py:56
  210.4 0.0 copy-done.1
  210.4 8.8 %fusion.11 = f32[64,128,128]{2,1,0:T(8,128)} fusion(f32[64,128,256]{2,1,0:T(8,128)} %reshape.22, f32[256,128,1]{1,0,2:T(8,128)S(1)} %copy-done.1), kind=kOutput, calls=%fused_computation.18 | convolution fusion | flops 1610612736 | bytes 12713984 | tf_op jit(solution)/shard_map/kqp,px->kqx/dot_general | solution.py:19
  219.2 5.4 %copy.35 = f32[64,128,128]{1,0,2:T(8,128)} copy(f32[64,128,128]{2,1,0:T(8,128)} %fusion.11) | data formatting | bytes 8388608 | tf_op jit(solution)/shard_map/kqp,px->kqx/dot_general | solution.py:19
  224.6 12.1 %all_to_all.81 = f32[64,128,128]{1,0,2:T(8,128)} all-to-all(f32[64,128,128]{1,0,2:T(8,128)} %copy.35), channel_id=1, replica_groups={{0,4},{8,12},{1,5},{9,13},{2,6},{10,14},{3,7},{11,15},{16,20},{24,28},{..., dimensions={2} | all-to-all | bytes 8388608 | tf_op jit(solution)/shard_map/all_to_all | solution.py:58
  236.7 5.4 %copy.36 = f32[64,128,128]{2,1,0:T(8,128)} copy(f32[64,128,128]{1,0,2:T(8,128)} %all_to_all.81) | data formatting | bytes 8388608 | tf_op jit(solution)/shard_map/all_to_all | solution.py:58
  242.1 7.0 %reshape.24 = f32[64,256,64]{2,1,0:T(8,128)} reshape(f32[64,128,128]{2,1,0:T(8,128)} %copy.36) | data formatting | bytes 8388608 | tf_op jit(solution)/shard_map/kqx,qy->kyx/dot_general | solution.py:19
  249.1 10.0 %convolution_bitcast_fusion.1 = f32[64,128,64]{1,2,0:T(8,128)S(1)} fusion(f32[64,256,64]{2,1,0:T(8,128)} %reshape.24, f32[256,128,1]{1,0,2:T(8,128)S(1)} %copy-done.6), kind=kOutput, calls=%fused_computation.7 | convolution fusion | flops 805306368 | bytes 6422528 | tf_op jit(solution)/shard_map/kqx,qy->kyx/dot_general | solution.py:19
  259.1 4.5 %copy.38 = f32[64,128,64]{2,0,1:T(8,128)} copy(f32[64,128,64]{1,2,0:T(8,128)S(1)} %convolution_bitcast_fusion.1) | data formatting | bytes 4194304 | tf_op jit(solution)/shard_map/kqx,qy->kyx/transpose | solution.py:19
  263.6 4.5 %reshape.45 = f32[4,1,131072]{2,1,0:T(1,128)S(1)} reshape(f32[128,64,64]{2,1,0:T(8,128)} %bitcast.55) | data formatting | bytes 4194304
  268.1 52.0 %all_to_all.82 = f32[4,1,131072]{2,1,0:T(1,128)} all-to-all(f32[4,1,131072]{2,1,0:T(1,128)S(1)} %reshape.45), channel_id=1, replica_groups=mesh['rep'=2,'px'=4,'py'=4] {'py'}, dimensions={0} | all-to-all | bytes 4194304 | tf_op jit(solution)/shard_map/all_to_all | solution.py:60
  320.1 7.7 %reduce.2 = f32[4,131072]{1,0:T(4,128)S(1)} reduce(f32[4,1,131072]{2,1,0:T(1,128)} %all_to_all.82, f32[]{:T(128)} %broadcast.3), dimensions={1}, to_apply=%all_to_all.68.reduce_sub_computation | reduce | bytes 4194308 | tf_op jit(solution)/shard_map/all_to_all | solution.py:60
  327.9 3.9 %reshape.46 = f32[128,64,64]{2,1,0:T(8,128)} reshape(f32[4,131072]{1,0:T(4,128)S(1)} %reduce.2) | data formatting | bytes 4194304
  331.8 4.7 %copy.39 = f32[64,128,64]{2,1,0:T(8,128)S(1)} copy(f32[64,128,64]{2,0,1:T(8,128)} %bitcast.59) | data formatting | bytes 4194304 | tf_op jit(solution)/shard_map/all_to_all | solution.py:60
  336.5 5.2 %fusion.2 = f32[32,64,128]{2,1,0:T(8,128)S(1)} fusion(f32[256,128,1]{1,0,2:T(8,128)S(1)} %copy-done.5, f32[256,32,64]{2,1,0:T(8,128)S(1)} %bitcast.57), kind=kOutput, calls=%fused_computation.3 | convolution fusion | flops 402653184 | bytes 3276800 | tf_op jit(solution)/shard_map/kyx,kz->xyz/dot_general | solution.py:19
  341.7 0.6 copy.41
  342.3 15.8 %all_to_all.83 = f32[2,32,32,128]{3,2,1,0:T(8,128)S(1)} all-to-all(f32[2,32,32,128]{3,2,1,0:T(8,128)S(1)} %copy.41), channel_id=1, replica_groups={{0,8},{4,12},{1,9},{5,13},{2,10},{6,14},{3,11},{7,15},{16,24},{20,28},{..., dimensions={0} | all-to-all | bytes 2097152 | tf_op jit(solution)/shard_map/all_to_all | solution.py:63
  358.1 1.0 copy.51
  (15 shorter events, 0.0 us)
Async XLA Ops:
  0.0 19.4 %copy-start.4 = (f32[256,128,1]{1,0,2:T(8,128)S(1)}, f32[256,128,1]{1,0,2:T(8,128)}, u32[]{:S(2)}) copy-start(f32[256,128,1]{1,0,2:T(8,128)} %constant.48) | copy-start | bytes 393220
  24.9 10.8 %copy-start.7 = (f32[3,89,256]{2,1,0:T(8,128)S(1)}, f32[3,89,256]{2,1,0:T(8,128)}, u32[]{:S(2)}) copy-start(f32[3,89,256]{2,1,0:T(8,128)} %param.10) | copy-start | bytes 820228
  24.9 10.8 %copy-start.8 = (f32[128]{0:T(128)S(1)}, f32[128]{0:T(128)}, u32[]{:S(2)}) copy-start(f32[128]{0:T(128)} %constant.39.clone) | copy-start | bytes 1540
  30.4 52.4 %all-to-all-start.1 = ((f32[4,1,131072]{2,1,0:T(1,128)}), f32[4,1,131072]{2,1,0:T(1,128)S(1)}, u32[]{:S(2)}, u32[]{:S(2)}) async-start(f32[4,1,131072]{2,1,0:T(1,128)} %reshape.41), calls=%async_computation.1 | async-start | bytes 4194304 | tf_op jit(solution)/shard_map/all_to_all | solution.py:49
  82.9 1.3 copy-start
  96.4 2.9 copy-start.3
  176.6 9.0 %copy-start.2 = (f32[2,128,128,1,1,1]{2,1,0,5,4,3:T(8,128)S(1)}, f32[2,128,128,1,1,1]{2,1,0,5,4,3:T(8,128)}, u32[]{:S(2)}) copy-start(f32[2,128,128,1,1,1]{2,1,0,5,4,3:T(8,128)} %constant.50) | copy-start | bytes 393220
  198.9 11.5 %copy-start.1 = (f32[256,128,1]{1,0,2:T(8,128)S(1)}, f32[256,128,1]{1,0,2:T(8,128)}, u32[]{:S(2)}) copy-start(f32[256,128,1]{1,0,2:T(8,128)} %constant.51) | copy-start | bytes 393220
  242.1 7.0 %copy-start.6 = (f32[256,128,1]{1,0,2:T(8,128)S(1)}, f32[256,128,1]{1,0,2:T(8,128)}, u32[]{:S(2)}) copy-start(f32[256,128,1]{1,0,2:T(8,128)} %constant.52) | copy-start | bytes 393220
  331.8 4.7 %copy-start.5 = (f32[256,128,1]{1,0,2:T(8,128)S(1)}, f32[256,128,1]{1,0,2:T(8,128)}, u32[]{:S(2)}) copy-start(f32[256,128,1]{1,0,2:T(8,128)} %constant.53) | copy-start | bytes 393220
where the time goes:
time: 365 us; the launch traced here: 360 us
  local copies, waits for them, and re-layouts  128 us (35%)
  blocking collectives  111 us (30%)
  waiting for transfers between devices  45.8 us (13%)
  matrix products  37.4 us (10%)
  other arithmetic  31.9 us (9%)
  starting transfers between devices  5.28 us (1%)
    all_to_all x1, blocking collectives, body(): held = lax.all_to_all(held, 'py', 1, 0, tiled=True)  52 us
    all_to_all x1, waiting for transfers between devices, body(): held = lax.all_to_all(held, 'py', 0, 1, tiled=True)  45.8 us
    unnamed x25, local copies, waits for them, and re-layouts  38.9 us
    dot_general x6, matrix products, dot(): jnp.einsum(spec, left, right, precision=HIGH, preferred_element_type=jnp....  36.5 us
    dot_general x3, local copies, waits for them, and re-layouts, dot(): jnp.einsum(spec, left, right, precision=HIGH, preferred_element_type=jnp....  21.4 us
    all_to_all x1, blocking collectives, body(): lax.all_to_all(density, 'px', 0, 0, axis_index_groups=trade, tiled=True)  18.8 us
    transpose x3, local copies, waits for them, and re-layouts, dot(): jnp.einsum(spec, left, right, precision=HIGH, preferred_element_type=jnp....  18.1 us
    all_to_all x1, other arithmetic, body(): held = lax.all_to_all(held, 'px', 1, 2, axis_index_groups=lines, tiled=True)  16.5 us
  transfers between devices with their start and end apart: 1, of which 1 were waited for; matrix products, arithmetic and copies ran while one was open for 0% of the time, Pallas kernels for 0%

commit v1 on v0

--- a/solution.py
+++ b/solution.py
@@ -46,7 +46,9 @@
     held = lax.all_to_all(density, "px", 0, 0, axis_index_groups=trade, tiled=True)
     held = held.reshape(replicas * rows_x, rows_y, length)
     held = dot("kz,xyz->kyx", table_z, held)
-    held = lax.all_to_all(held, "py", 0, 1, tiled=True)
+    held = jnp.concatenate(
+        lax.all_to_all(jnp.stack(jnp.split(held, lax.axis_size("py"), axis=0)), "py", 0, 0), axis=1
+    )
     held = dot("qy,kyx->kqx", table_y, held)
     held = lax.all_to_all(held, "px", 1, 2, axis_index_groups=lines, tiled=True)
     z_freq, y_freq = (length // count_py, length // half)

time: 365 us -> 363 us (level)
    reshape x0 -> x1, local copies, waits for them, and re-layouts: none -> 4.95 us  [body(): jnp.concatenate(lax.all_to_all(jnp.stack(jnp.split(held, lax.axis_size('p...]
    transpose x3 -> x2, local copies, waits for them, and re-layouts: 18.1 us -> 13.6 us  [dot(): jnp.einsum(spec, left, right, precision=HIGH, preferred_element_type=jnp....]
where the time goes in v1:
time: 363 us; the launch traced here: 358 us
  local copies, waits for them, and re-layouts  126 us (35%)
  blocking collectives  111 us (31%)
  waiting for transfers between devices  45.9 us (13%)
  matrix products  35.3 us (10%)
  other arithmetic  34.3 us (9%)
  starting transfers between devices  5.3 us (1%)
    all_to_all x1, blocking collectives, body(): held = lax.all_to_all(held, 'py', 1, 0, tiled=True)  52 us
    all_to_all x1, waiting for transfers between devices, body(): lax.all_to_all(jnp.stack(jnp.split(held, lax.axis_size('py'), axis=0)), '...  45.9 us
    unnamed x25, local copies, waits for them, and re-layouts  38.9 us
    dot_general x6, matrix products, dot(): jnp.einsum(spec, left, right, precision=HIGH, preferred_element_type=jnp....  34.3 us
    dot_general x3, local copies, waits for them, and re-layouts, dot(): jnp.einsum(spec, left, right, precision=HIGH, preferred_element_type=jnp....  21.4 us
    all_to_all x1, blocking collectives, body(): lax.all_to_all(density, 'px', 0, 0, axis_index_groups=trade, tiled=True)  18.8 us
    all_to_all x1, other arithmetic, body(): held = lax.all_to_all(held, 'px', 1, 2, axis_index_groups=lines, tiled=True)  16.5 us
    all_to_all x1, blocking collectives, body(): return lax.all_to_all(held, 'px', 0, 0, axis_index_groups=trade, tiled=True)  15.8 us
  transfers between devices with their start and end apart: 1, of which 1 were waited for; matrix products, arithmetic and copies ran while one was open for 0% of the time, Pallas kernels for 0%

profile of v1, /device:TPU:0, one launch (start us, length us, event | category | flops | bytes accessed | tf_op | source)
XLA Modules:
  0.0 358.3 jit_solution(18320046844317106124)
XLA Ops:
  0.0 18.8 %all_to_all.66 = f32[2,32,32,128]{3,2,1,0:T(8,128)S(1)} all-to-all(f32[2,32,32,128]{3,2,1,0:T(8,128)} %param.9), channel_id=1, replica_groups={{0,8},{4,12},{1,9},{5,13},{2,10},{6,14},{3,11},{7,15},{16,24},{20,28},{..., dimensions={0} | all-to-all | bytes 2097152 | tf_op jit(solution)/shard_map/all_to_all | solution.py:46
  18.8 0.6 copy.25
  19.4 0.0 copy-done.4
  19.4 1.0 convolution_bitcast_fusion.2
  20.4 0.8 slice_bitcast_fusion.3
  21.2 2.4 fusion.11
  23.6 5.5 %reshape.49 = f32[4,1,131072]{2,1,0:T(1,128)} reshape(f32[4,32,64,64]{3,2,1,0:T(8,128)} %fusion.11) | data formatting | bytes 4194304
  29.2 5.3 %all-to-all-start.1 = ((f32[4,1,131072]{2,1,0:T(1,128)}), f32[4,1,131072]{2,1,0:T(1,128)S(1)}, u32[]{:S(2)}, u32[]{:S(2)}) async-start(f32[4,1,131072]{2,1,0:T(1,128)} %reshape.49), calls=%async_computation.1 | async-start | bytes 4194304 | tf_op jit(solution)/shard_map/all_to_all | solution.py:50
  34.5 0.0 copy-done.7
  34.5 0.0 copy-done.8
  34.5 0.1 constant_dynamic-slice_fusion.1
  34.6 0.1 copy.29
  34.7 0.1 constant_dynamic-slice_fusion
  34.8 0.1 copy.30
  34.9 1.0 fusion.6
  35.9 45.9 %all-to-all-done.1 = f32[4,1,131072]{2,1,0:T(1,128)S(1)} async-done(((f32[4,1,131072]{2,1,0:T(1,128)}), f32[4,1,131072]{2,1,0:T(1,128)S(1)}, u32[]{:S(2)}, u32[]{:S(2)}) %all-to-all-start.1) | async-done | bytes 2097184 | tf_op jit(solution)/shard_map/all_to_all | solution.py:50
  81.8 1.3 copy-done
  83.1 0.5 broadcast.3
  83.6 7.7 %reduce = f32[4,131072]{1,0:T(4,128)S(1)} reduce(f32[4,1,131072]{2,1,0:T(1,128)} %copy-done, f32[]{:T(128)} %broadcast.3), dimensions={1}, to_apply=%all_to_all.47.reduce_sub_computation | reduce | bytes 4194308 | tf_op jit(solution)/shard_map/all_to_all | solution.py:50
  91.3 3.9 %reshape.50 = f32[4,32,64,64]{3,2,1,0:T(8,128)} reshape(f32[4,131072]{1,0:T(4,128)S(1)} %reduce) | data formatting | bytes 4194304
  95.3 5.0 %copy.26 = f32[64,128,64]{1,2,0:T(8,128)S(1)} copy(f32[64,128,64]{0,2,1:T(8,128)} %bitcast.65) | data formatting | bytes 4194304 | tf_op jit(solution)/shard_map/reshape | solution.py:49
  100.2 3.7 %convolution_bitcast_fusion = f32[64,256,64]{1,2,0:T(8,128)} fusion(f32[64,128,64]{1,2,0:T(8,128)S(1)} %copy.26, f32[256,128,1]{1,0,2:T(8,128)S(1)} %copy-done.3), kind=kOutput, calls=%fused_computation.7 | convolution fusion | flops 805306368 | bytes 6422528 | tf_op jit(solution)/shard_map/qy,kyx->kqx/dot_general | solution.py:19
  104.0 9.1 %copy.27 = f32[64,256,64]{2,0,1:T(8,128)} copy(f32[64,256,64]{1,2,0:T(8,128)} %convolution_bitcast_fusion) | data formatting | bytes 8388608 | tf_op jit(solution)/shard_map/qy,kyx->kqx/transpose | solution.py:19
  113.1 8.7 %reshape.51 = f32[2,1,524288]{2,1,0:T(1,128)} reshape(f32[256,64,64]{2,1,0:T(8,128)} %bitcast.62) | data formatting | bytes 8388608
  121.8 11.9 %all_to_all.67 = f32[2,1,524288]{2,1,0:T(1,128)} all-to-all(f32[2,1,524288]{2,1,0:T(1,128)} %reshape.51), channel_id=1, replica_groups={{0,4},{8,12},{1,5},{9,13},{2,6},{10,14},{3,7},{11,15},{16,20},{24,28},{..., dimensions={0} | all-to-all | bytes 8388608 | tf_op jit(solution)/shard_map/all_to_all | solution.py:53
  133.7 16.5 %reduce.1 = f32[2,524288]{1,0:T(2,128)} reduce(f32[2,1,524288]{2,1,0:T(1,128)} %all_to_all.67, f32[]{:T(128)} %broadcast.3), dimensions={1}, to_apply=%all_to_all.48.reduce_sub_computation | reduce | bytes 8388612 | tf_op jit(solution)/shard_map/all_to_all | solution.py:53
  150.1 9.9 %reshape.52 = f32[256,64,64]{2,1,0:T(8,128)} reshape(f32[2,524288]{1,0:T(2,128)} %reduce.1) | data formatting | bytes 8388608
  160.1 15.3 %copy.45 = f32[64,2,128,64]{3,1,2,0:T(2,128)} copy(f32[64,2,128,64]{3,0,2,1:T(8,128)} %bitcast.63) | data formatting | bytes 8388608 | tf_op jit(solution)/shard_map/all_to_all | solution.py:53
  175.4 9.0 %reshape.42 = f32[2,32,2,64,128,1]{4,3,2,1,0,5:T(8,128)} reshape(f32[64,128,2,64]{3,2,1,0:T(2,128)} %bitcast.64) | data formatting | bytes 8388608 | tf_op jit(solution)/shard_map/kqx,px->kqp/dot_general | solution.py:19
  184.4 5.6 %broadcast_multiply_fusion = f32[2,32,2,64,2,128]{5,3,4,2,1,0:T(8,128)S(1)} fusion(f32[32,64,128]{2,1,0:T(8,128)S(1)} %fusion.6, f32[2,128,128,1,1,1]{2,1,0,5,4,3:T(8,128)S(1)} %copy-done.2, f32[2,32,2,64,128,1]{4,3,2,1,0,5:T(8,128)} %reshape.42), kind=kOutput, calls=%fused_computation.6 | convolution fusion | flops 1612709888 | bytes 13762560 | tf_op jit(solution)/shard_map/kqx,px->kqp/dot_general | solution.py:19
  189.9 7.7 %copy.31 = f32[2,32,2,64,2,128]{5,4,3,2,1,0:T(2,128)} copy(f32[2,32,2,64,2,128]{5,3,4,2,1,0:T(8,128)S(1)} %broadcast_multiply_fusion) | data formatting | bytes 16777216 | tf_op jit(solution)/shard_map/mul | solution.py:57
  197.7 11.5 %reshape.30 = f32[64,128,256]{2,1,0:T(8,128)} reshape(f32[2,32,2,64,2,128]{5,4,3,2,1,0:T(2,128)} %copy.31) | data formatting | bytes 16777216 | tf_op jit(solution)/shard_map/reshape | solution.py:58
  209.2 8.8 %fusion.12 = f32[64,128,128]{2,1,0:T(8,128)} fusion(f32[64,128,256]{2,1,0:T(8,128)} %reshape.30, f32[256,128,1]{1,0,2:T(8,128)S(1)} %copy-done.1), kind=kOutput, calls=%fused_computation.24 | convolution fusion | flops 1610612736 | bytes 12713984 | tf_op jit(solution)/shard_map/kqp,px->kqx/dot_general | solution.py:19
  217.9 5.4 %copy.32 = f32[64,128,128]{1,0,2:T(8,128)} copy(f32[64,128,128]{2,1,0:T(8,128)} %fusion.12) | data formatting | bytes 8388608 | tf_op jit(solution)/shard_map/kqp,px->kqx/dot_general | solution.py:19
  223.4 12.0 %all_to_all.68 = f32[64,128,128]{1,0,2:T(8,128)} all-to-all(f32[64,128,128]{1,0,2:T(8,128)} %copy.32), channel_id=1, replica_groups={{0,4},{8,12},{1,5},{9,13},{2,6},{10,14},{3,7},{11,15},{16,20},{24,28},{..., dimensions={2} | all-to-all | bytes 8388608 | tf_op jit(solution)/shard_map/all_to_all | solution.py:60
  235.4 5.4 %copy.33 = f32[64,128,128]{2,1,0:T(8,128)} copy(f32[64,128,128]{1,0,2:T(8,128)} %all_to_all.68) | data formatting | bytes 8388608 | tf_op jit(solution)/shard_map/all_to_all | solution.py:60
  240.8 7.0 %reshape.32 = f32[64,256,64]{2,1,0:T(8,128)} reshape(f32[64,128,128]{2,1,0:T(8,128)} %copy.33) | data formatting | bytes 8388608 | tf_op jit(solution)/shard_map/kqx,qy->kyx/dot_general | solution.py:19
  247.8 10.0 %convolution_bitcast_fusion.1 = f32[64,128,64]{1,2,0:T(8,128)S(1)} fusion(f32[64,256,64]{2,1,0:T(8,128)} %reshape.32, f32[256,128,1]{1,0,2:T(8,128)S(1)} %copy-done.6), kind=kOutput, calls=%fused_computation.8 | convolution fusion | flops 805306368 | bytes 6422528 | tf_op jit(solution)/shard_map/kqx,qy->kyx/dot_general | solution.py:19
  257.9 4.5 %copy.35 = f32[64,128,64]{2,0,1:T(8,128)} copy(f32[64,128,64]{1,2,0:T(8,128)S(1)} %convolution_bitcast_fusion.1) | data formatting | bytes 4194304 | tf_op jit(solution)/shard_map/kqx,qy->kyx/transpose | solution.py:19
  262.3 4.5 %reshape.53 = f32[4,1,131072]{2,1,0:T(1,128)S(1)} reshape(f32[128,64,64]{2,1,0:T(8,128)} %bitcast.66) | data formatting | bytes 4194304
  266.9 52.0 %all_to_all.69 = f32[4,1,131072]{2,1,0:T(1,128)} all-to-all(f32[4,1,131072]{2,1,0:T(1,128)S(1)} %reshape.53), channel_id=1, replica_groups=mesh['rep'=2,'px'=4,'py'=4] {'py'}, dimensions={0} | all-to-all | bytes 4194304 | tf_op jit(solution)/shard_map/all_to_all | solution.py:62
  318.9 7.7 %reduce.2 = f32[4,131072]{1,0:T(4,128)S(1)} reduce(f32[4,1,131072]{2,1,0:T(1,128)} %all_to_all.69, f32[]{:T(128)} %broadcast.3), dimensions={1}, to_apply=%all_to_all.55.reduce_sub_computation | reduce | bytes 4194308 | tf_op jit(solution)/shard_map/all_to_all | solution.py:62
  326.6 3.9 %reshape.54 = f32[128,64,64]{2,1,0:T(8,128)} reshape(f32[4,131072]{1,0:T(4,128)S(1)} %reduce.2) | data formatting | bytes 4194304
  330.5 4.7 %copy.36 = f32[64,128,64]{2,1,0:T(8,128)S(1)} copy(f32[64,128,64]{2,0,1:T(8,128)} %bitcast.68) | data formatting | bytes 4194304 | tf_op jit(solution)/shard_map/all_to_all | solution.py:62
  335.2 5.2 %fusion.2 = f32[32,64,128]{2,1,0:T(8,128)S(1)} fusion(f32[256,128,1]{1,0,2:T(8,128)S(1)} %copy-done.5, f32[256,32,64]{2,1,0:T(8,128)S(1)} %bitcast.67), kind=kOutput, calls=%fused_computation.4 | convolution fusion | flops 402653184 | bytes 3276800 | tf_op jit(solution)/shard_map/kyx,kz->xyz/dot_general | solution.py:19
  340.4 0.6 copy.38
  341.0 15.8 %all_to_all.70 = f32[2,32,32,128]{3,2,1,0:T(8,128)S(1)} all-to-all(f32[2,32,32,128]{3,2,1,0:T(8,128)S(1)} %copy.38), channel_id=1, replica_groups={{0,8},{4,12},{1,9},{5,13},{2,10},{6,14},{3,11},{7,15},{16,24},{20,28},{..., dimensions={0} | all-to-all | bytes 2097152 | tf_op jit(solution)/shard_map/all_to_all | solution.py:65
  356.8 1.0 copy.47
  (16 shorter events, 0.0 us)
Async XLA Ops:
  0.0 19.4 %copy-start.4 = (f32[256,128,1]{1,0,2:T(8,128)S(1)}, f32[256,128,1]{1,0,2:T(8,128)}, u32[]{:S(2)}) copy-start(f32[256,128,1]{1,0,2:T(8,128)} %constant.48) | copy-start | bytes 393220
  23.6 10.9 %copy-start.7 = (f32[3,89,256]{2,1,0:T(8,128)S(1)}, f32[3,89,256]{2,1,0:T(8,128)}, u32[]{:S(2)}) copy-start(f32[3,89,256]{2,1,0:T(8,128)} %param.10) | copy-start | bytes 820228
  23.6 10.9 %copy-start.8 = (f32[128]{0:T(128)S(1)}, f32[128]{0:T(128)}, u32[]{:S(2)}) copy-start(f32[128]{0:T(128)} %constant.39.clone) | copy-start | bytes 1540
  29.2 52.6 %all-to-all-start.1 = ((f32[4,1,131072]{2,1,0:T(1,128)}), f32[4,1,131072]{2,1,0:T(1,128)S(1)}, u32[]{:S(2)}, u32[]{:S(2)}) async-start(f32[4,1,131072]{2,1,0:T(1,128)} %reshape.49), calls=%async_computation.1 | async-start | bytes 4194304 | tf_op jit(solution)/shard_map/all_to_all | solution.py:50
  81.8 1.3 copy-start
  95.3 5.0 %copy-start.3 = (f32[256,128,1]{1,0,2:T(8,128)S(1)}, f32[256,128,1]{1,0,2:T(8,128)}, u32[]{:S(2)}) copy-start(f32[256,128,1]{1,0,2:T(8,128)} %constant.49) | copy-start | bytes 393220
  175.4 9.0 %copy-start.2 = (f32[2,128,128,1,1,1]{2,1,0,5,4,3:T(8,128)S(1)}, f32[2,128,128,1,1,1]{2,1,0,5,4,3:T(8,128)}, u32[]{:S(2)}) copy-start(f32[2,128,128,1,1,1]{2,1,0,5,4,3:T(8,128)} %constant.50) | copy-start | bytes 393220
  197.7 11.5 %copy-start.1 = (f32[256,128,1]{1,0,2:T(8,128)S(1)}, f32[256,128,1]{1,0,2:T(8,128)}, u32[]{:S(2)}) copy-start(f32[256,128,1]{1,0,2:T(8,128)} %constant.51) | copy-start | bytes 393220
  240.8 7.0 %copy-start.6 = (f32[256,128,1]{1,0,2:T(8,128)S(1)}, f32[256,128,1]{1,0,2:T(8,128)}, u32[]{:S(2)}) copy-start(f32[256,128,1]{1,0,2:T(8,128)} %constant.52) | copy-start | bytes 393220
  330.5 4.7 %copy-start.5 = (f32[256,128,1]{1,0,2:T(8,128)S(1)}, f32[256,128,1]{1,0,2:T(8,128)}, u32[]{:S(2)}) copy-start(f32[256,128,1]{1,0,2:T(8,128)} %constant.53) | copy-start | bytes 393220
